TPU v7x, 32 devices: a whole 2x2x4 slice. The times are simulated.
32 devices in a mesh: groups: 2 (over y), expert: 4 (over x, core), cuts: 4 (over z).
Axes of the slice: x: 2, y: 2, z: 4, core: 2. Of those that a mesh axis runs over, the one named last changes fastest.
Arguments:
- tokens: bfloat16 [4096, 2048], P(('groups', 'expert')), parts along dimension 0, may hold values from -6 to 6
- route: int32 [4096, 1], P(('groups', 'expert')), parts along dimension 0, may hold values from 0 to 3; in each aligned block of 512 rows (0 to 511, 512 to 1023, ...) at most 192 rows name the same one
- gate_prob: float32 [4096], P(('groups', 'expert')), parts along dimension 0, may hold values from 0.2 to 1
- norm_gain: float32 [2048], replicated, may hold values from 0.5 to 1.5
- dense_in: bfloat16 [2048, 8192], P('expert', 'cuts'), may hold values from -0.125 to 0.125
- dense_out: bfloat16 [8192, 2048], P('cuts', 'expert'), may hold values from -0.0625 to 0.0625
- expert_in: bfloat16 [4, 2048, 8192], P('expert', None, 'cuts'), may hold values from -0.125 to 0.125
- expert_out: bfloat16 [4, 8192, 2048], P('expert', 'cuts'), may hold values from -0.0625 to 0.0625
Outputs:
- layer_out: bfloat16 [4096, 2048], P(('groups', 'expert'), 'cuts'), parts along dimension 0
There are 2 independent parts, one for each index of `groups`. A program takes and returns all parts, laid end to end along the dimension named above; an argument that names none is the same for every part. Nothing has to cross between parts.
Inputs may be any that keep to these rules, and one draw needn't show every extreme that they name: `route`: within the rows of one device (aligned blocks of 512 rows) no expert is named by more than 192 rows; in some blocks one expert is named by exactly 192 rows.
All inputs are finite; a program needn't handle non-finite values.
Results may differ from a plain program's by a relative error of at most 0.0095.
Values may be sent and summed in bfloat16 or wider, within the bound.
A program may use at most 128 MiB of HBM per device.

v0:
```python
import jax
import jax.numpy as jnp
from jax import lax
from jax.sharding import PartitionSpec as P


def normalize(tokens, norm_gain):
    widened = tokens.astype(jnp.float32)
    meansq = jnp.mean(widened * widened, axis=-1, keepdims=True)
    return (widened * lax.rsqrt(meansq + 1e-06) * norm_gain).astype(jnp.bfloat16)


def residual_mlp(normed, dense_in, dense_out):
    before_act = jnp.dot(
        normed,
        lax.all_gather(dense_in, "expert", axis=0, tiled=True),
        preferred_element_type=jnp.float32,
    )
    dense_act = jax.nn.gelu(before_act).astype(jnp.bfloat16)
    partial_out = jnp.dot(
        dense_act,
        lax.all_gather(dense_out, "expert", axis=1, tiled=True),
        preferred_element_type=jnp.float32,
    )
    return lax.psum_scatter(
        partial_out.astype(jnp.bfloat16), "cuts", scatter_dimension=1, tiled=True
    ).astype(jnp.float32)


def local(tokens, route, gate_prob, norm_gain, dense_in, dense_out, expert_in, expert_out):
    experts = lax.axis_size("expert")
    slices = lax.axis_size("cuts")
    tok_rows, width = tokens.shape
    share = width // slices
    capacity = max(2, 3 * tok_rows // (2 * experts))
    normed = normalize(tokens, norm_gain)
    dense = residual_mlp(normed, dense_in, dense_out)
    picked = route[:, 0]
    labels = jnp.arange(experts, dtype=jnp.int32)
    one_hot = (picked[:, None] == labels[None, :]).astype(jnp.int32)
    before = jnp.cumsum(one_hot, axis=0) - one_hot
    position = jnp.sum(before * one_hot, axis=-1)
    target = picked * capacity + position
    outgoing = jnp.zeros((experts * capacity, width), jnp.bfloat16).at[target].set(normed)
    outgoing = outgoing.reshape(experts, capacity, width)
    weight_in = expert_in[0]
    weight_out = expert_out[0]
    arrived = lax.all_to_all(outgoing, "expert", split_axis=0, concat_axis=0, tiled=True)
    sources = arrived.shape[0]
    count = arrived.shape[1]
    flat_rows = arrived.reshape(sources * count, width)
    inner = jax.nn.gelu(jnp.dot(flat_rows, weight_in, preferred_element_type=jnp.float32)).astype(
        jnp.bfloat16
    )
    partial_res = jnp.dot(inner, weight_out, preferred_element_type=jnp.float32).reshape(
        sources, count, width
    )
    cut_index = lax.axis_index("cuts")
    own_share = lax.psum_scatter(
        partial_res.astype(jnp.bfloat16), "cuts", scatter_dimension=2, tiled=True
    )
    returned = lax.all_to_all(own_share, "expert", split_axis=0, concat_axis=0, tiled=True)
    expert_res = returned.reshape(experts * capacity, share)[target].astype(jnp.float32)
    own_tokens = lax.dynamic_slice_in_dim(tokens, cut_index * share, share, 1).astype(jnp.float32)
    layer_out = own_tokens + dense + gate_prob[:, None] * expert_res
    return layer_out.astype(jnp.bfloat16)


def solution(mesh):
    return jax.shard_map(
        local,
        mesh=mesh,
        in_specs=(
            P(("groups", "expert"), None),
            P(("groups", "expert"), None),
            P(("groups", "expert")),
            P(),
            P("expert", "cuts"),
            P("cuts", "expert"),
            P("expert", None, "cuts"),
            P("expert", "cuts", None),
        ),
        out_specs=P(("groups", "expert"), "cuts"),
        check_vma=False,
    )
```

profile of v0, /device:TPU:0, one launch (start us, length us, event | category | flops | bytes accessed | tf_op | source)
XLA Modules:
  0.0 233.7 jit_solution(18360485246939992458)
XLA Ops:
  7.4 0.7 all-gather.3.cloned.1.call-update
  8.1 0.0 all-gather.5.cloned.1.call-start
  8.1 0.7 all-gather.5.cloned.1.call-update
  8.8 0.0 reduce-scatter.5.cloned.1.call-start
  8.9 1.2 reduce-window.6
  10.1 0.2 slice_reduce_fusion
  10.4 0.2 reduce-window.9
  10.5 0.1 add_bitcast_fusion
  10.7 0.5 fusion.12
  11.2 5.9 %scatter_custom_fusion = bf16[768,2048]{1,0:T(8,128)(2,1)S(1)} fusion(s32[512]{0:T(512)S(1)} %bitcast.52, bf16[]{:T(256)} %constant.9.clone.1, bf16[512,2048]{1,0:T(8,128)(2,1)} %param.8, f32[2048]{0:T(1024)S(1)} %copy-done.3, f32[512]{0:T(512)S(1)} %add_rsqrt_fusion), kind=kCustom, calls=%fused_computation.35 | custom fusion | flops 4194304 | bytes 5253122 | tf_op jit(solution)/shard_map/scatter | solution.py:44
  17.1 75.1 %all_to_all.10 = bf16[4,192,2048]{2,1,0:T(8,128)(2,1)S(1)} all-to-all(bf16[4,192,2048]{2,1,0:T(8,128)(2,1)S(1)} %bitcast.48), channel_id=1, replica_groups=mesh['groups'=2,'expert'=4,'cuts'=4] {'expert'}, dimensions={0} | all-to-all | bytes 6291456 | tf_op jit(solution)/shard_map/all_to_all | solution.py:48
  92.2 10.4 %fusion.11 = bf16[768,2048]{1,0:T(8,128)(2,1)S(1)} fusion(bf16[768,2048]{1,0:T(8,128)(2,1)S(1)} %bitcast.49, bf16[1,2048,2048]{2,1,0:T(8,128)(2,1)} %param.14), kind=kOutput, calls=%fused_computation.14 | convolution fusion | flops 6456606720 | bytes 14680064 | tf_op jit(solution)/shard_map/dot_general | solution.py:52
  102.6 8.0 %fusion.25 = bf16[4,192,2048]{2,1,0:T(8,128)(2,1)} fusion(bf16[4,192,2048]{2,1,0:T(8,128)(2,1)S(1)} %bitcast.58, bf16[1,2048,2048]{2,1,0:T(8,128)(2,1)S(1)} %bitcast.57), kind=kOutput, calls=%fused_computation.29 | convolution fusion | flops 6444023808 | bytes 14680064 | tf_op jit(solution)/shard_map/dot_general | solution.py:55
  110.6 0.0 reduce-scatter.5.cloned.1.call-update
  110.7 0.2 reduce-scatter.3.cloned.1.call-start
  110.9 0.0 all-gather.3.cloned.1.call-done
  110.9 53.4 %all-gather.5.cloned.1.call-done = bf16[2048,2048]{1,0:T(8,128)(2,1)} async-done(((bf16[2048,512]{1,0:T(8,128)(2,1)}), bf16[2048,2048]{1,0:T(8,128)(2,1)}) %all-gather.5.cloned.1.call-update) | async-done | bytes 8388624 | tf_op jit(solution)/shard_map/all_gather | solution.py:22
  164.3 16.1 %convolution_convert_fusion = bf16[512,2048]{1,0:T(8,128)(2,1)} fusion(bf16[2048,2048]{1,0:T(8,128)(2,1)} %all-gather.5.cloned.1.call-done, bf16[2048,2048]{1,0:T(8,128)(2,1)} %all-gather.3.cloned.1.call-done, bf16[512,2048]{1,0:T(8,128)(2,1)S(1)} %copy-done.1, f32[2048]{0:T(1024)S(1)} %copy-done.3, f32[512]{0:T(512)S(1)} %add_rsqrt_fusion), kind=kOutput, calls=%fused_computation.30 | convolution fusion | flops 8604614656 | bytes 20981760 | tf_op jit(solution)/shard_map/dot_general | solution.py:20
  180.5 0.0 reduce-scatter.5.cloned.1.call-done
  180.5 3.5 %all-to-all-start.1 = ((bf16[4,192,512]{2,1,0:T(8,128)(2,1)}), bf16[4,192,512]{2,1,0:T(8,128)(2,1)S(1)}, u32[]{:S(2)}, u32[]{:S(2)}) async-start(bf16[4,192,512]{2,1,0:T(8,128)(2,1)} %reduce-scatter.5.cloned.1.call-done), calls=%async_computation.3 | async-start | bytes 1572864 | tf_op jit(solution)/shard_map/all_to_all | solution.py:62
  184.0 11.6 %all-to-all-done.1 = bf16[4,192,512]{2,1,0:T(8,128)(2,1)S(1)} async-done(((bf16[4,192,512]{2,1,0:T(8,128)(2,1)}), bf16[4,192,512]{2,1,0:T(8,128)(2,1)S(1)}, u32[]{:S(2)}, u32[]{:S(2)}) %all-to-all-start.1) | async-done | bytes 786464 | tf_op jit(solution)/shard_map/all_to_all | solution.py:62
  195.6 2.0 gather_fusion
  197.6 26.6 %reduce-scatter.3.cloned.1.call-done = bf16[512,512]{1,0:T(8,128)(2,1)} async-done(((bf16[512,2048]{1,0:T(8,128)(2,1)}), bf16[512,512]{1,0:T(8,128)(2,1)}) %reduce-scatter.3.cloned.1.call-update) | async-done | bytes 524304 | tf_op jit(solution)/shard_map/reduce_scatter | solution.py:25
  224.2 2.1 add_convert_fusion
  (22 shorter events, 0.1 us)
Async XLA Ops:
  7.4 1.5 copy-start.2
  7.4 3.3 %copy-start = (bf16[512,2048]{1,0:T(8,128)(2,1)S(1)}, bf16[512,2048]{1,0:T(8,128)(2,1)}, u32[]{:S(2)}) copy-start(bf16[512,2048]{1,0:T(8,128)(2,1)} %param.8) | copy-start | bytes 6291460
  7.4 3.8 %copy-start.3 = (f32[2048]{0:T(1024)S(1)}, f32[2048]{0:T(1024)}, u32[]{:S(2)}) copy-start(f32[2048]{0:T(1024)} %param.11) | copy-start | bytes 24580
  7.4 103.6 %all-gather.3.cloned.1.call-start = ((), (), s32[]{:S(2)}) async-start(), calls=%async_computation.4 | async-start | bytes 10485760 | tf_op jit(solution)/shard_map/all_gather | solution.py:16
  8.1 156.2 %all-gather.5.cloned.1.call-start = ((), (), s32[]{:S(2)}) async-start(), calls=%async_computation.5 | async-start | bytes 10485760 | tf_op jit(solution)/shard_map/all_gather | solution.py:22
  8.8 171.6 %reduce-scatter.5.cloned.1.call-start = ((), (), s32[]{:S(2)}) async-start(), calls=%async_computation.7 | async-start | bytes 3932160 | tf_op jit(solution)/shard_map/reduce_scatter | solution.py:59
  17.0 85.5 %slice-start = ((s8[8388608]{0:T(1024)(128)(4,1)}), s8[4194304]{0:T(1024)(128)(4,1)S(1)}, s32[]{:S(2)}) async-start(s8[8388608]{0:T(1024)(128)(4,1)} %bitcast.56), calls=%async_computation.8 | async-start | bytes 8388608
  92.2 10.4 %slice-start.1 = ((s8[8388608]{0:T(1024)(128)(4,1)}), s8[4194304]{0:T(1024)(128)(4,1)S(1)}, s32[]{:S(2)}) async-start(s8[8388608]{0:T(1024)(128)(4,1)} %bitcast.56), calls=%async_computation.9 | async-start | bytes 8388608
  102.6 61.7 %copy-start.1 = (bf16[512,2048]{1,0:T(8,128)(2,1)S(1)}, bf16[512,2048]{1,0:T(8,128)(2,1)}, u32[]{:S(2)}) copy-start(bf16[512,2048]{1,0:T(8,128)(2,1)} %param.8) | copy-start | bytes 6291460
  110.7 113.5 %reduce-scatter.3.cloned.1.call-start = ((), (), s32[]{:S(2)}) async-start(), calls=%async_computation.6 | async-start | bytes 2621440 | tf_op jit(solution)/shard_map/reduce_scatter | solution.py:25
  180.4 43.8 %copy-start.4 = (f32[512]{0:T(512)S(1)}, f32[512]{0:T(512)}, u32[]{:S(2)}) copy-start(f32[512]{0:T(512)} %param.10) | copy-start | bytes 6148
  180.5 15.1 %all-to-all-start.1 = ((bf16[4,192,512]{2,1,0:T(8,128)(2,1)}), bf16[4,192,512]{2,1,0:T(8,128)(2,1)S(1)}, u32[]{:S(2)}, u32[]{:S(2)}) async-start(bf16[4,192,512]{2,1,0:T(8,128)(2,1)} %reduce-scatter.5.cloned.1.call-done), calls=%async_computation.3 | async-start | bytes 1572864 | tf_op jit(solution)/shard_map/all_to_all | solution.py:62
Sparse Core Ops, SparseCore 0:
  9.7 94.6 all-gather.2
  106.0 58.2 all-gather.4
Sparse Core Ops, SparseCore 1:
  110.8 60.9 reduce-scatter.4
  180.5 43.6 reduce-scatter.2
where the time goes:
time: 234 us
  waiting for transfers between devices  93.1 us (40%)
  blocking collectives  75.1 us (32%)
  matrix products  34.5 us (15%)
  between operations  15 us (6%)
  other arithmetic  9.96 us (4%)
  starting transfers between devices  3.81 us (2%)
    all_to_all x1, blocking collectives, local(): lax.all_to_all(outgoing, 'expert', split_axis=0, concat_axis=0, tiled=True)  75.1 us
    all_gather x1, waiting for transfers between devices, residual_mlp(): lax.all_gather(dense_out, 'expert', axis=1, tiled=True)  53.4 us
    reduce_scatter x1, waiting for transfers between devices, residual_mlp(): lax.psum_scatter(partial_out.astype(jnp.bfloat16), 'cuts', scatter_dimens...  26.6 us
    dot_general x1, matrix products, residual_mlp(): jnp.dot(dense_act, lax.all_gather(dense_out, 'expert', axis=1, tiled=True...  16.1 us
    all_to_all x1, waiting for transfers between devices, local(): lax.all_to_all(own_share, 'expert', split_axis=0, concat_axis=0, tiled=True)  11.6 us
    dot_general x1, matrix products, local(): jnp.dot(flat_rows, weight_in, preferred_element_type=jnp.float32)  10.4 us
    dot_general x1, matrix products, local(): jnp.dot(inner, weight_out, preferred_element_type=jnp.float32)  8.04 us
    scatter x1, other arithmetic, local(): jnp.zeros((experts * capacity, width), jnp.bfloat16).at[target].set(normed)  5.86 us
  transfers between devices with their start and end apart: 5, of which 3 were waited for; matrix products, arithmetic and copies ran while one was open for 19% of the time, Pallas kernels for 0%

commit v1 on v0

v1 whole, which is shorter than its diff:
```python
import functools

import jax
import jax.numpy as jnp
from jax import lax
from jax.experimental import pallas as pl
from jax.experimental.pallas import tpu as pltpu
from jax.sharding import PartitionSpec as P

SUB = 4


def kernel(G, E, Z, cap, tokens, route, gate, gain, din, dout, ein_h, eout_h, out,
           win, wout, ein, eout, tok, normed, disp, arrived, hbuf, pe, rpe, pd, rpd, ret, rret,
           loc, own_s, own_r, disp_s, disp_r, wx_s, wx_r, wy_s, wy_r, wp_s, wp_r,
           ze_s, ze_r, zd_s, zd_r, ret_s, ret_r):
    f32, bf16 = jnp.float32, jnp.bfloat16
    T, D = tok.shape
    F = ein.shape[1]
    De = D // E
    share = D // Z
    C = E // 2
    pair = 2 * cap
    tn = min(256, share)
    g, e, z = lax.axis_index("groups"), lax.axis_index("expert"), lax.axis_index("cuts")
    chip, core = e // 2, lax.rem(e, 2)
    partner = chip * 2 + 1 - core

    def remote(src, dst, send, recv, gg=None, ee=None, zz=None):
        return pltpu.make_async_remote_copy(
            src_ref=src, dst_ref=dst, send_sem=send, recv_sem=recv,
            device_id={
                "groups": g if gg is None else gg,
                "expert": e if ee is None else ee,
                "cuts": z if zz is None else zz,
            },
            device_id_type=pl.DeviceIdType.MESH,
        )

    def expert_at(kc, j):
        other = lax.rem(chip + kc + C, C)
        return other * 2 + (core if j == 0 else 1 - core)

    barrier = pltpu.get_barrier_semaphore()
    for k in range(1, E):
        pl.semaphore_signal(barrier, inc=1, device_id={"groups": g, "expert": lax.rem(e + k, E), "cuts": z},
                            device_id_type=pl.DeviceIdType.MESH)
    for k in range(1, Z):
        pl.semaphore_signal(barrier, inc=1, device_id={"groups": g, "expert": e, "cuts": lax.rem(z + k, Z)},
                            device_id_type=pl.DeviceIdType.MESH)
    for k in range(1, G):
        pl.semaphore_signal(barrier, inc=1, device_id={"groups": lax.rem(g + k, G), "expert": e, "cuts": z},
                            device_id_type=pl.DeviceIdType.MESH)

    my_rows = pl.ds(pl.multiple_of(e * De, De), De)
    locals_ = [
        pltpu.make_async_copy(tokens, tok, loc.at[0]),
        pltpu.make_async_copy(ein_h.at[0], ein, loc.at[1]),
        pltpu.make_async_copy(eout_h.at[0], eout, loc.at[2]),
        pltpu.make_async_copy(din, win.at[my_rows, :], loc.at[3]),
        pltpu.make_async_copy(dout, wout.at[:, my_rows], loc.at[4]),
    ]
    for copy in locals_:
        copy.start()
    locals_[0].wait()

    nrow = min(64, T)

    def norm_step(i, carry):
        rows = pl.ds(pl.multiple_of(i * nrow, nrow), nrow)
        x = tok[rows, :].astype(f32)
        ms = jnp.mean(x * x, axis=-1, keepdims=True)
        normed[rows, :] = (x * lax.rsqrt(ms + 1e-06) * gain[...]).astype(bf16)
        return carry

    lax.fori_loop(0, T // nrow, norm_step, 0)

    picked = route[...]
    one_hot = (lax.broadcasted_iota(jnp.int32, (T, 128), 1) == picked).astype(f32)
    lower = (lax.broadcasted_iota(jnp.int32, (T, T), 1) < lax.broadcasted_iota(jnp.int32, (T, T), 0))
    before = jnp.dot(lower.astype(f32).astype(bf16), one_hot.astype(bf16), preferred_element_type=f32)
    position = jnp.sum(before * one_hot, axis=1, keepdims=True)
    slot_col = picked.astype(f32) * float(cap) + position
    slot_row = jnp.transpose(jnp.broadcast_to(slot_col, (T, 128)))[0:1, :]

    pl.semaphore_wait(barrier, (E - 1) + (Z - 1) + (G - 1))

    own_copies = [
        remote(din, win.at[my_rows, :], own_s.at[0], own_r.at[0], ee=partner),
        remote(dout, wout.at[:, my_rows], own_s.at[1], own_r.at[1], ee=partner),
    ]

    def fill(q, dst):
        dest = expert_at(q // 2, q % 2)
        wanted = slot_row - (dest * cap).astype(f32)
        pick = (lax.broadcasted_iota(jnp.int32, (cap, T), 0).astype(f32) == wanted).astype(f32).astype(bf16)
        dn = min(512, D)

        def step(i, carry):
            cols = pl.ds(pl.multiple_of(i * dn, dn), dn)
            dst[q * cap:(q + 1) * cap, cols] = jnp.dot(
                pick, normed[:, cols], preferred_element_type=f32).astype(bf16)
            return carry

        lax.fori_loop(0, D // dn, step, 0)

    def disp_copy(q):
        return remote(disp.at[pl.ds(q * cap, cap), :], arrived.at[pl.ds(q * cap, cap), :],
                      disp_s.at[q], disp_r.at[q], ee=expert_at(q // 2, q % 2))

    order = list(range(2, E)) + [1]
    pending = None
    for q in order:
        fill(q, disp)
        if pending is not None:
            disp_copy(pending).start()
        pending = q
    fill(0, arrived)
    disp_copy(pending).start()

    def in_at(owner, p, s):
        n = De // G // SUB
        return pl.ds(pl.multiple_of(owner * De + p * (De // G) + s * n, n), n)

    def weight(m, owner, p, s):
        if m == 0:
            n = De // G // SUB
            return win.at[pl.ds(pl.multiple_of(owner * De + p * (De // G) + s * n, n), n), :]
        n = F // G // SUB
        return wout.at[pl.ds(pl.multiple_of(p * (F // G) + s * n, n), n),
                       pl.ds(pl.multiple_of(owner * De, De), De)]

    def weight_source(m, p, s):
        ref, rows = (din, De) if m == 0 else (dout, F)
        n = rows // G // SUB
        return ref.at[pl.ds(pl.multiple_of(p * (rows // G) + s * n, n), n), :]

    def x_copy(m, kc, s):
        return remote(weight_source(m, g, s), weight(m, e, g, s), wx_s.at[m, kc, s], wx_r.at[m, kc, s],
                      ee=expert_at(kc, 0))

    def y_copy(m, kc, s, dg):
        w = weight(m, expert_at(-kc, 0), g, s)
        return remote(w, w, wy_s.at[m, kc, s, dg], wy_r.at[m, kc, s, dg], gg=lax.rem(g + dg, G))

    def p_copy(m, kc, s, dg):
        w = weight(m, expert_at(-kc, 0), lax.rem(g - dg + G, G), s)
        return remote(w, w, wp_s.at[m, kc, s, dg], wp_r.at[m, kc, s, dg], ee=partner)

    for m in range(2):
        for s in range(SUB):
            for kc in range(1, C):
                x_copy(m, kc, s).start()
    for copy in own_copies:
        copy.start()

    def ze_copy(kc, r):
        rows = pl.ds(kc * pair, pair)
        return remote(pe.at[r, rows, :], rpe.at[r, rows, :], ze_s.at[kc, r], ze_r.at[kc, r],
                      zz=lax.rem(z + r, Z))

    def zd_copy(r):
        return remote(pd.at[r], rpd.at[r], zd_s.at[r], zd_r.at[r], zz=lax.rem(z + r, Z))

    def hidden(load, rows, w):
        def step(i, carry):
            cols = pl.ds(pl.multiple_of(i * 256, 256), 256)
            acc = jnp.dot(load(), w[:, cols], preferred_element_type=f32)
            hbuf[0:rows, cols] = jax.nn.gelu(acc).astype(bf16)
            return carry

        lax.fori_loop(0, F // 256, step, 0)

    def partials(rows, w, store, send):
        late = None
        for r in list(range(Z - 1, 0, -1)) + [0]:
            base = lax.rem(z + r, Z) * share

            def step(i, carry):
                cols = pl.ds(pl.multiple_of(base + i * tn, tn), tn)
                acc = jnp.dot(hbuf[0:rows, :], w[:, cols], preferred_element_type=f32)
                store(r, pl.ds(pl.multiple_of(i * tn, tn), tn), acc.astype(bf16))
                return carry

            lax.fori_loop(0, share // tn, step, 0)
            if late is not None:
                send(late).start()
            late = r

    locals_[1].wait()
    locals_[2].wait()
    for kc in range(C):
        for q in (2 * kc, 2 * kc + 1):
            if q:
                disp_copy(q).wait_recv()
        lo = kc * pair
        hidden(lambda: arrived[lo:lo + pair, :], pair, ein)

        def store(r, cols, value):
            pe[r, lo:lo + pair, cols] = value

        partials(pair, eout, store, lambda r: ze_copy(kc, r))

    def forward(m):
        for s in range(SUB):
            for kc in range(1, C):
                x_copy(m, kc, s).wait_recv()
                for dg in range(1, G):
                    y_copy(m, kc, s, dg).start()
                p_copy(m, kc, s, 0).start()
            if s:
                forward_group(m, s - 1)
        forward_group(m, SUB - 1)

    def forward_group(m, s):
        for kc in range(1, C):
            for dg in range(1, G):
                y_copy(m, kc, s, dg).wait_recv()
                p_copy(m, kc, s, dg).start()

    def collect(m):
        locals_[3 + m].wait()
        own_copies[m].wait_recv()
        for s in range(SUB):
            for kc in range(1, C):
                for dg in range(G):
                    p_copy(m, kc, s, dg).wait_recv()

    forward(0)
    collect(0)
    hidden(lambda: normed[...], T, win)
    forward(1)
    collect(1)

    def store_dense(r, cols, value):
        pd[r, :, cols] = value

    partials(T, wout, store_dense, zd_copy)

    def ret_copy(q):
        return remote(ret.at[pl.ds(q * cap, cap), :], rret.at[pl.ds(q * cap, cap), :],
                      ret_s.at[q], ret_r.at[q], ee=expert_at(-(q // 2), q % 2))

    for kc in list(range(1, C)) + [0]:
        lo = kc * pair
        for r in range(1, Z):
            ze_copy(kc, r).wait_recv()
        for q in (2 * kc + 1, 2 * kc):
            rows = slice(q * cap, (q + 1) * cap)
            total = pe[0, rows, :].astype(f32)
            for r in range(1, Z):
                total = total + rpe[r, rows, :].astype(f32)
            if q:
                ret[rows, :] = total.astype(bf16)
            else:
                rret[rows, :] = total.astype(bf16)
        for q in (2 * kc, 2 * kc + 1):
            if q:
                ret_copy(q).start()

    for q in range(1, E):
        ret_copy(q).wait_recv()

    for r in range(1, Z):
        zd_copy(r).wait_recv()

    trow = min(128, T)
    residual = pl.ds(pl.multiple_of(z * share, share), share)
    for i in range(T // trow):
        rows = slice(i * trow, (i + 1) * trow)
        res = jnp.zeros((trow, share), f32)
        for q in range(E):
            wanted = slot_col[rows, :] - (expert_at(q // 2, q % 2) * cap).astype(f32)
            pick = (lax.broadcasted_iota(jnp.int32, (trow, cap), 1).astype(f32) == wanted).astype(f32).astype(bf16)
            res = res + jnp.dot(pick, rret[q * cap:(q + 1) * cap, :], preferred_element_type=f32)
        dense = pd[0, rows, :].astype(f32)
        for r in range(1, Z):
            dense = dense + rpd[r, rows, :].astype(f32)
        out[rows, :] = (tok[rows, residual].astype(f32) + dense + gate[rows, :] * res).astype(bf16)

    for copy in own_copies:
        copy.wait_send()
    for q in range(1, E):
        disp_copy(q).wait_send()
        ret_copy(q).wait_send()
    for m in range(2):
        for s in range(SUB):
            for kc in range(1, C):
                x_copy(m, kc, s).wait_send()
                for dg in range(1, G):
                    y_copy(m, kc, s, dg).wait_send()
                for dg in range(G):
                    p_copy(m, kc, s, dg).wait_send()
    for r in range(1, Z):
        for kc in range(C):
            ze_copy(kc, r).wait_send()
        zd_copy(r).wait_send()


def local(tokens, route, gate_prob, norm_gain, dense_in, dense_out, expert_in, expert_out):
    G, E, Z = lax.axis_size("groups"), lax.axis_size("expert"), lax.axis_size("cuts")
    T, D = tokens.shape
    F = dense_in.shape[1]
    share = D // Z
    cap = max(2, 3 * T // (2 * E))
    C = E // 2
    bf16 = jnp.bfloat16
    any_, vmem = pl.BlockSpec(memory_space=pl.ANY), pl.BlockSpec(memory_space=pltpu.VMEM)
    dma = pltpu.SemaphoreType.DMA
    return pl.pallas_call(
        functools.partial(kernel, G, E, Z, cap),
        out_shape=jax.ShapeDtypeStruct((T, share), bf16),
        in_specs=[any_, vmem, vmem, vmem, any_, any_, any_, any_],
        out_specs=vmem,
        scratch_shapes=[
            pltpu.VMEM((D, F), bf16), pltpu.VMEM((F, D), bf16),
            pltpu.VMEM((D, F), bf16), pltpu.VMEM((F, D), bf16),
            pltpu.VMEM((T, D), bf16), pltpu.VMEM((T, D), bf16),
            pltpu.VMEM((E * cap, D), bf16), pltpu.VMEM((E * cap, D), bf16),
            pltpu.VMEM((max(T, 2 * cap), F), bf16),
            pltpu.VMEM((Z, E * cap, share), bf16), pltpu.VMEM((Z, E * cap, share), bf16),
            pltpu.VMEM((Z, T, share), bf16), pltpu.VMEM((Z, T, share), bf16),
            pltpu.VMEM((E * cap, share), bf16), pltpu.VMEM((E * cap, share), bf16),
            dma((5,)), dma((2,)), dma((2,)), dma((E,)), dma((E,)),
            dma((2, C, SUB)), dma((2, C, SUB)),
            dma((2, C, SUB, G)), dma((2, C, SUB, G)), dma((2, C, SUB, G)), dma((2, C, SUB, G)),
            dma((C, Z)), dma((C, Z)), dma((Z,)), dma((Z,)), dma((E,)), dma((E,)),
        ],
        compiler_params=pltpu.CompilerParams(
            collective_id=0, has_side_effects=True, vmem_limit_bytes=67043328
        ),
    )(tokens, route, gate_prob[:, None], norm_gain[None, :], dense_in, dense_out, expert_in, expert_out)


def solution(mesh):
    return jax.shard_map(
        local,
        mesh=mesh,
        in_specs=(
            P(("groups", "expert"), None),
            P(("groups", "expert"), None),
            P(("groups", "expert")),
            P(),
            P("expert", "cuts"),
            P("cuts", "expert"),
            P("expert", None, "cuts"),
            P("expert", "cuts", None),
        ),
        out_specs=P(("groups", "expert"), "cuts"),
        check_vma=False,
    )
```

time: 234 us -> 170 us (0.73)
  Pallas kernels: 0 us -> 165 us
  waiting for transfers between devices: 93.1 us -> 0 us
  blocking collectives: 75.1 us -> 0 us
  matrix products: 34.5 us -> 0 us
  between operations: 15 us -> 0.01 us
  other arithmetic: 9.96 us -> 0 us
  starting transfers between devices: 3.81 us -> 0 us
  local copies, waits for them, and re-layouts: 2.21 us -> 4.94 us
    pallas_call x0 -> x1, Pallas kernels: none -> 165 us  [local(): pl.pallas_call(functools.partial(kernel, G, E, Z, cap), out_shape=jax.Sha...]
    all_to_all x1 -> x0, blocking collectives: 75.1 us -> none  [local(): lax.all_to_all(outgoing, 'expert', split_axis=0, concat_axis=0, tiled=True)]
    all_gather x2 -> x0, waiting for transfers between devices: 53.4 us -> none  [the longest x1 53.4 us: residual_mlp(): lax.all_gather(dense_out, 'expert', axis=1, tiled=True)]
    dot_general x3 -> x0, matrix products: 34.5 us -> none  [the longest x1 16.1 us: residual_mlp(): jnp.dot(dense_act, lax.all_gather(dense_out, 'expert', axis=1, tiled=True...]
    reduce_scatter x2 -> x0, waiting for transfers between devices: 26.6 us -> none  [the longest x1 26.6 us: residual_mlp(): lax.psum_scatter(partial_out.astype(jnp.bfloat16), 'cuts', scatter_dimens...]
    all_to_all x1 -> x0, waiting for transfers between devices: 11.6 us -> none  [local(): lax.all_to_all(own_share, 'expert', split_axis=0, concat_axis=0, tiled=True)]
    scatter x1 -> x0, other arithmetic: 5.86 us -> none  [local(): jnp.zeros((experts * capacity, width), jnp.bfloat16).at[target].set(normed)]
    all_to_all x1 -> x0, starting transfers between devices: 3.5 us -> none  [local(): lax.all_to_all(own_share, 'expert', split_axis=0, concat_axis=0, tiled=True)]
  transfers between devices with their start and end apart: 5 -> 0, of which waited for: 3 -> 0; matrix products, arithmetic and copies ran while one was open for 19% -> 0% of each run, Pallas kernels for 0% -> 0%
where the time goes in v1:
time: 170 us
  Pallas kernels  165 us (97%)
  local copies, waits for them, and re-layouts  4.94 us (3%)
    pallas_call x1, Pallas kernels, local(): pl.pallas_call(functools.partial(kernel, G, E, Z, cap), out_shape=jax.Sha...  165 us
    unnamed x2, local copies, waits for them, and re-layouts  3.4 us

profile of v1, /device:TPU:0, one launch (start us, length us, event | category | flops | bytes accessed | tf_op | source)
XLA Modules:
  0.0 169.7 jit_solution(17509220948877131083)
XLA Ops:
  0.0 1.5 copy.10.route
  1.5 1.5 copy.11.gate
  3.1 164.7 %shard_map.82 = bf16[512,512]{1,0:T(8,128)(2,1)} custom-call(bf16[512,2048]{1,0:T(8,128)(2,1)} %tokens.1, s32[512,1]{1,0:T(8,128)} %copy.10.route, f32[512,1]{1,0:T(8,128)} %copy.11.gate, f32[1,2048]{1,0:T(1,128)} %bitcast.2, bf16[512,2048]{1,0:T(8,128)(2,1)} %din.1, bf16[2048,512]{1,0:T(8,128)(2,1)} %dout.1, bf16[1,2048,2048]{2,1,0:T(8,128)(2,1)} %ein_h.1, ...), custom_call_target="tpu_custom_call" | custom-call | tf_op jit(solution)/shard_map/pallas_call | solution.py:310
  167.8 1.9 %copy.13 = bf16[512,512]{1,0:T(8,128)(2,1)} copy(bf16[512,512]{1,0:T(8,128)(2,1)} %shard_map.82) | data formatting | bytes 1048576

commit v2 on v1

--- a/solution.py
+++ b/solution.py
@@ -7,7 +7,9 @@
 from jax.experimental.pallas import tpu as pltpu
 from jax.sharding import PartitionSpec as P
 
-SUB = 4
+SUBS = (4, 4)
+WINDOW = 3
+EARLY = 1
 
 
 def kernel(G, E, Z, cap, tokens, route, gate, gain, din, dout, ein_h, eout_h, out,
@@ -62,6 +64,72 @@
     ]
     for copy in locals_:
         copy.start()
+    pl.semaphore_wait(barrier, (E - 1) + (Z - 1) + (G - 1))
+
+    own_copies = [
+        remote(din, win.at[my_rows, :], own_s.at[0], own_r.at[0], ee=partner),
+        remote(dout, wout.at[:, my_rows], own_s.at[1], own_r.at[1], ee=partner),
+    ]
+
+    def weight(m, owner, p, s):
+        if m == 0:
+            n = De // G // SUBS[m]
+            return win.at[pl.ds(pl.multiple_of(owner * De + p * (De // G) + s * n, n), n), :]
+        n = F // G // SUBS[m]
+        return wout.at[pl.ds(pl.multiple_of(p * (F // G) + s * n, n), n),
+                       pl.ds(pl.multiple_of(owner * De, De), De)]
+
+    def weight_source(m, p, s):
+        ref, rows = (din, De) if m == 0 else (dout, F)
+        n = rows // G // SUBS[m]
+        return ref.at[pl.ds(pl.multiple_of(p * (rows // G) + s * n, n), n), :]
+
+    def x_copy(m, kc, s):
+        return remote(weight_source(m, g, s), weight(m, e, g, s), wx_s.at[m, kc, s], wx_r.at[m, kc, s],
+                      ee=expert_at(kc, 0))
+
+    def y_copy(m, kc, s, dg):
+        w = weight(m, expert_at(-kc, 0), g, s)
+        return remote(w, w, wy_s.at[m, kc, s, dg], wy_r.at[m, kc, s, dg], gg=lax.rem(g + dg, G))
+
+    def p_copy(m, kc, s, dg):
+        w = weight(m, expert_at(-kc, 0), lax.rem(g - dg + G, G), s)
+        return remote(w, w, wp_s.at[m, kc, s, dg], wp_r.at[m, kc, s, dg], ee=partner)
+
+    steps = [(m, s) for m in range(2) for s in range(SUBS[m])]
+    issued, taken, relayed = [0], [0], [0]
+
+    def issue(upto):
+        while issued[0] < min(upto, len(steps)):
+            m, s = steps[issued[0]]
+            for kc in range(1, C):
+                x_copy(m, kc, s).start()
+            issued[0] += 1
+
+    def relay():
+        m, s = steps[relayed[0]]
+        for kc in range(1, C):
+            for dg in range(1, G):
+                y_copy(m, kc, s, dg).wait_recv()
+                p_copy(m, kc, s, dg).start()
+        relayed[0] += 1
+
+    def take(upto):
+        while taken[0] < min(upto, len(steps)):
+            m, s = steps[taken[0]]
+            for kc in range(1, C):
+                x_copy(m, kc, s).wait_recv()
+            if taken[0] >= EARLY:
+                issue(taken[0] + 1 + WINDOW)
+            for kc in range(1, C):
+                for dg in range(1, G):
+                    y_copy(m, kc, s, dg).start()
+                p_copy(m, kc, s, 0).start()
+            if relayed[0] < taken[0]:
+                relay()
+            taken[0] += 1
+
+    issue(EARLY)
     locals_[0].wait()
 
     nrow = min(64, T)
@@ -82,13 +150,6 @@
     position = jnp.sum(before * one_hot, axis=1, keepdims=True)
     slot_col = picked.astype(f32) * float(cap) + position
     slot_row = jnp.transpose(jnp.broadcast_to(slot_col, (T, 128)))[0:1, :]
-
-    pl.semaphore_wait(barrier, (E - 1) + (Z - 1) + (G - 1))
-
-    own_copies = [
-        remote(din, win.at[my_rows, :], own_s.at[0], own_r.at[0], ee=partner),
-        remote(dout, wout.at[:, my_rows], own_s.at[1], own_r.at[1], ee=partner),
-    ]
 
     def fill(q, dst):
         dest = expert_at(q // 2, q % 2)
@@ -118,39 +179,6 @@
     fill(0, arrived)
     disp_copy(pending).start()
 
-    def in_at(owner, p, s):
-        n = De // G // SUB
-        return pl.ds(pl.multiple_of(owner * De + p * (De // G) + s * n, n), n)
-
-    def weight(m, owner, p, s):
-        if m == 0:
-            n = De // G // SUB
-            return win.at[pl.ds(pl.multiple_of(owner * De + p * (De // G) + s * n, n), n), :]
-        n = F // G // SUB
-        return wout.at[pl.ds(pl.multiple_of(p * (F // G) + s * n, n), n),
-                       pl.ds(pl.multiple_of(owner * De, De), De)]
-
-    def weight_source(m, p, s):
-        ref, rows = (din, De) if m == 0 else (dout, F)
-        n = rows // G // SUB
-        return ref.at[pl.ds(pl.multiple_of(p * (rows // G) + s * n, n), n), :]
-
-    def x_copy(m, kc, s):
-        return remote(weight_source(m, g, s), weight(m, e, g, s), wx_s.at[m, kc, s], wx_r.at[m, kc, s],
-                      ee=expert_at(kc, 0))
-
-    def y_copy(m, kc, s, dg):
-        w = weight(m, expert_at(-kc, 0), g, s)
-        return remote(w, w, wy_s.at[m, kc, s, dg], wy_r.at[m, kc, s, dg], gg=lax.rem(g + dg, G))
-
-    def p_copy(m, kc, s, dg):
-        w = weight(m, expert_at(-kc, 0), lax.rem(g - dg + G, G), s)
-        return remote(w, w, wp_s.at[m, kc, s, dg], wp_r.at[m, kc, s, dg], ee=partner)
-
-    for m in range(2):
-        for s in range(SUB):
-            for kc in range(1, C):
-                x_copy(m, kc, s).start()
     for copy in own_copies:
         copy.start()
 
@@ -159,17 +187,23 @@
         return remote(pe.at[r, rows, :], rpe.at[r, rows, :], ze_s.at[kc, r], ze_r.at[kc, r],
                       zz=lax.rem(z + r, Z))
 
-    def zd_copy(r):
-        return remote(pd.at[r], rpd.at[r], zd_s.at[r], zd_r.at[r], zz=lax.rem(z + r, Z))
-
-    def hidden(load, rows, w):
+    halfrows = T // 2
+
+    def zd_copy(d, slot, c, to):
+        rows = pl.ds(c * halfrows, halfrows)
+        return remote(pd.at[d, rows, :], rpd.at[slot, rows, :], zd_s.at[d, c], zd_r.at[slot, c], zz=to)
+
+    def back_slot(d, to):
+        return Z if d == to else d
+
+    def hidden(load, rows, w, lo=0, hi=None):
         def step(i, carry):
             cols = pl.ds(pl.multiple_of(i * 256, 256), 256)
             acc = jnp.dot(load(), w[:, cols], preferred_element_type=f32)
             hbuf[0:rows, cols] = jax.nn.gelu(acc).astype(bf16)
             return carry
 
-        lax.fori_loop(0, F // 256, step, 0)
+        lax.fori_loop(lo, F // 256 if hi is None else hi, step, 0)
 
     def partials(rows, w, store, send):
         late = None
@@ -193,6 +227,8 @@
         for q in (2 * kc, 2 * kc + 1):
             if q:
                 disp_copy(q).wait_recv()
+        if kc == C - 1:
+            issue(EARLY + WINDOW)
         lo = kc * pair
         hidden(lambda: arrived[lo:lo + pair, :], pair, ein)
 
@@ -200,42 +236,52 @@
             pe[r, lo:lo + pair, cols] = value
 
         partials(pair, eout, store, lambda r: ze_copy(kc, r))
-
-    def forward(m):
-        for s in range(SUB):
-            for kc in range(1, C):
-                x_copy(m, kc, s).wait_recv()
-                for dg in range(1, G):
-                    y_copy(m, kc, s, dg).start()
-                p_copy(m, kc, s, 0).start()
-            if s:
-                forward_group(m, s - 1)
-        forward_group(m, SUB - 1)
-
-    def forward_group(m, s):
-        for kc in range(1, C):
-            for dg in range(1, G):
-                y_copy(m, kc, s, dg).wait_recv()
-                p_copy(m, kc, s, dg).start()
+        if kc == 0:
+            take(EARLY)
 
     def collect(m):
         locals_[3 + m].wait()
         own_copies[m].wait_recv()
-        for s in range(SUB):
+        for s in range(SUBS[m]):
             for kc in range(1, C):
                 for dg in range(G):
                     p_copy(m, kc, s, dg).wait_recv()
 
-    forward(0)
+    first = SUBS[0]
+    take(first + 1)
+    while relayed[0] < first:
+        relay()
     collect(0)
-    hidden(lambda: normed[...], T, win)
-    forward(1)
+    blocks = F // 256
+    for part in range(4):
+        hidden(lambda: normed[...], T, win, part * blocks // 4, (part + 1) * blocks // 4)
+        take(first + 2 + part)
+    take(len(steps))
+    while relayed[0] < len(steps):
+        relay()
     collect(1)
 
-    def store_dense(r, cols, value):
-        pd[r, :, cols] = value
-
-    partials(T, wout, store_dense, zd_copy)
+    upper = (2 * z) // Z
+    for i in range(Z):
+        d = (1 - upper) * (Z - 1 - i) + upper * i
+
+        def dense_step(k, carry):
+            cols = pl.ds(pl.multiple_of(d * share + k * tn, tn), tn)
+            acc = jnp.dot(hbuf[0:T, :], wout[:, cols], preferred_element_type=f32)
+            pd[d, :, pl.ds(pl.multiple_of(k * tn, tn), tn)] = acc.astype(bf16)
+            return carry
+
+        lax.fori_loop(0, share // tn, dense_step, 0)
+        if i < Z - 1:
+            @pl.when(z == 0)
+            def _():
+                for c in range(2):
+                    zd_copy(Z - 1 - i, Z - 1 - i, c, 1).start()
+
+            @pl.when(z == Z - 1)
+            def _():
+                for c in range(2):
+                    zd_copy(i, back_slot(i, Z - 2), c, Z - 2).start()
 
     def ret_copy(q):
         return remote(ret.at[pl.ds(q * cap, cap), :], rret.at[pl.ds(q * cap, cap), :],
@@ -258,11 +304,51 @@
             if q:
                 ret_copy(q).start()
 
+    def add_arrived(d, c):
+        rows = slice(c * halfrows, (c + 1) * halfrows)
+        pd[d, rows, :] = (pd[d, rows, :].astype(f32) + rpd[d, rows, :].astype(f32)).astype(bf16)
+
+    for t in range(Z - 1):
+        for c in range(2):
+            up, down = Z - 1 - t, t
+
+            @pl.when((z > 0) & (z < up))
+            def _():
+                zd_copy(up, up, c, lax.rem(z + 1, Z)).wait_recv()
+                add_arrived(up, c)
+                zd_copy(up, up, c, lax.rem(z + 1, Z)).start()
+
+            @pl.when((z < Z - 1) & (z > down + 1))
+            def _():
+                zd_copy(down, down, c, lax.rem(z + Z - 1, Z)).wait_recv()
+                add_arrived(down, c)
+                zd_copy(down, down, c, lax.rem(z + Z - 1, Z)).start()
+
+            @pl.when((z < Z - 1) & (z == down + 1))
+            def _():
+                zd_copy(down, down, c, lax.rem(z + Z - 1, Z)).wait_recv()
+                add_arrived(down, c)
+                zd_copy(down, Z, c, lax.rem(z + Z - 1, Z)).start()
+
     for q in range(1, E):
         ret_copy(q).wait_recv()
 
-    for r in range(1, Z):
-        zd_copy(r).wait_recv()
+    @pl.when(z == 0)
+    def _():
+        rpd[0] = jnp.zeros((T, share), bf16)
+
+    @pl.when(z == Z - 1)
+    def _():
+        rpd[Z] = jnp.zeros((T, share), bf16)
+
+    for c in range(2):
+        @pl.when(z > 0)
+        def _():
+            zd_copy(z, z, c, lax.rem(z + 1, Z)).wait_recv()
+
+        @pl.when(z < Z - 1)
+        def _():
+            zd_copy(z, Z, c, lax.rem(z + 1, Z)).wait_recv()
 
     trow = min(128, T)
     residual = pl.ds(pl.multiple_of(z * share, share), share)
@@ -273,9 +359,7 @@
             wanted = slot_col[rows, :] - (expert_at(q // 2, q % 2) * cap).astype(f32)
             pick = (lax.broadcasted_iota(jnp.int32, (trow, cap), 1).astype(f32) == wanted).astype(f32).astype(bf16)
             res = res + jnp.dot(pick, rret[q * cap:(q + 1) * cap, :], preferred_element_type=f32)
-        dense = pd[0, rows, :].astype(f32)
-        for r in range(1, Z):
-            dense = dense + rpd[r, rows, :].astype(f32)
+        dense = pd[z, rows, :].astype(f32) + rpd[z, rows, :].astype(f32) + rpd[Z, rows, :].astype(f32)
         out[rows, :] = (tok[rows, residual].astype(f32) + dense + gate[rows, :] * res).astype(bf16)
 
     for copy in own_copies:
@@ -284,7 +368,7 @@
         disp_copy(q).wait_send()
         ret_copy(q).wait_send()
     for m in range(2):
-        for s in range(SUB):
+        for s in range(SUBS[m]):
             for kc in range(1, C):
                 x_copy(m, kc, s).wait_send()
                 for dg in range(1, G):
@@ -294,7 +378,11 @@
     for r in range(1, Z):
         for kc in range(C):
             ze_copy(kc, r).wait_send()
-        zd_copy(r).wait_send()
+    for d in range(Z):
+        @pl.when(z != d)
+        def _():
+            for c in range(2):
+                zd_copy(d, d, c, lax.rem(z + 1, Z)).wait_send()
 
 
 def local(tokens, route, gate_prob, norm_gain, dense_in, dense_out, expert_in, expert_out):
@@ -319,12 +407,12 @@
             pltpu.VMEM((E * cap, D), bf16), pltpu.VMEM((E * cap, D), bf16),
             pltpu.VMEM((max(T, 2 * cap), F), bf16),
             pltpu.VMEM((Z, E * cap, share), bf16), pltpu.VMEM((Z, E * cap, share), bf16),
-            pltpu.VMEM((Z, T, share), bf16), pltpu.VMEM((Z, T, share), bf16),
+            pltpu.VMEM((Z, T, share), bf16), pltpu.VMEM((Z + 1, T, share), bf16),
             pltpu.VMEM((E * cap, share), bf16), pltpu.VMEM((E * cap, share), bf16),
             dma((5,)), dma((2,)), dma((2,)), dma((E,)), dma((E,)),
-            dma((2, C, SUB)), dma((2, C, SUB)),
-            dma((2, C, SUB, G)), dma((2, C, SUB, G)), dma((2, C, SUB, G)), dma((2, C, SUB, G)),
-            dma((C, Z)), dma((C, Z)), dma((Z,)), dma((Z,)), dma((E,)), dma((E,)),
+            dma((2, C, max(SUBS))), dma((2, C, max(SUBS))),
+            dma((2, C, max(SUBS), G)), dma((2, C, max(SUBS), G)), dma((2, C, max(SUBS), G)), dma((2, C, max(SUBS), G)),
+            dma((C, Z)), dma((C, Z)), dma((Z, 2)), dma((Z + 1, 2)), dma((E,)), dma((E,)),
         ],
         compiler_params=pltpu.CompilerParams(
             collective_id=0, has_side_effects=True, vmem_limit_bytes=67043328

time: 170 us -> 156 us (0.918)
  the two profiles are of different devices: /device:TPU:0 before, /device:TPU:20 now
where the time goes in v2:
time: 156 us
  Pallas kernels  151 us (97%)
  local copies, waits for them, and re-layouts  4.94 us (3%)
    pallas_call x1, Pallas kernels, local(): pl.pallas_call(functools.partial(kernel, G, E, Z, cap), out_shape=jax.Sha...  151 us
    unnamed x2, local copies, waits for them, and re-layouts  3.4 us

profile of v2, /device:TPU:20, one launch (start us, length us, event | category | flops | bytes accessed | tf_op | source)
XLA Modules:
  0.0 155.6 jit_solution(10880500036667649609)
XLA Ops:
  0.0 1.5 copy.10.route
  1.5 1.5 copy.11.gate
  3.1 150.6 %shard_map.82 = bf16[512,512]{1,0:T(8,128)(2,1)} custom-call(bf16[512,2048]{1,0:T(8,128)(2,1)} %tokens.1, s32[512,1]{1,0:T(8,128)} %copy.10.route, f32[512,1]{1,0:T(8,128)} %copy.11.gate, f32[1,2048]{1,0:T(1,128)} %bitcast.2, bf16[512,2048]{1,0:T(8,128)(2,1)} %din.1, bf16[2048,512]{1,0:T(8,128)(2,1)} %dout.1, bf16[1,2048,2048]{2,1,0:T(8,128)(2,1)} %ein_h.1, ...), custom_call_target="tpu_custom_call" | custom-call | tf_op jit(solution)/shard_map/pallas_call | solution.py:398
  153.7 1.9 %copy.13 = bf16[512,512]{1,0:T(8,128)(2,1)} copy(bf16[512,512]{1,0:T(8,128)(2,1)} %shard_map.82) | data formatting | bytes 1048576

commit v3 on v2

--- a/solution.py
+++ b/solution.py
@@ -13,7 +13,7 @@
 
 
 def kernel(G, E, Z, cap, tokens, route, gate, gain, din, dout, ein_h, eout_h, out,
-           win, wout, ein, eout, tok, normed, disp, arrived, hbuf, pe, rpe, pd, rpd, ret, rret,
+           win, wout, ein, eout, tok, normed, disp, arrived, hbuf, pe, rpe, pd, rpd, ret, rret, base,
            loc, own_s, own_r, disp_s, disp_r, wx_s, wx_r, wy_s, wy_r, wp_s, wp_r,
            ze_s, ze_r, zd_s, zd_r, ret_s, ret_r):
     f32, bf16 = jnp.float32, jnp.bfloat16
@@ -308,30 +308,56 @@
         rows = slice(c * halfrows, (c + 1) * halfrows)
         pd[d, rows, :] = (pd[d, rows, :].astype(f32) + rpd[d, rows, :].astype(f32)).astype(bf16)
 
+    trow = min(128, T)
+    residual = pl.ds(pl.multiple_of(z * share, share), share)
+
+    def combine_experts():
+        for q in range(1, E):
+            ret_copy(q).wait_recv()
+        for i in range(T // trow):
+            rows = slice(i * trow, (i + 1) * trow)
+            res = jnp.zeros((trow, share), f32)
+            for q in range(E):
+                wanted = slot_col[rows, :] - (expert_at(q // 2, q % 2) * cap).astype(f32)
+                pick = (lax.broadcasted_iota(jnp.int32, (trow, cap), 1).astype(f32) == wanted)
+                res = res + jnp.dot(pick.astype(f32).astype(bf16), rret[q * cap:(q + 1) * cap, :],
+                                    preferred_element_type=f32)
+            base[rows, :] = tok[rows, residual].astype(f32) + gate[rows, :] * res
+
+    above, below = lax.rem(z + 1, Z), lax.rem(z + Z - 1, Z)
+
+    def pass_up(d, c):
+        @pl.when((z > 0) & (z < d))
+        def _():
+            zd_copy(d, d, c, above).wait_recv()
+            add_arrived(d, c)
+            zd_copy(d, d, c, above).start()
+
+    def pass_down(d, c):
+        for slot, near in ((d, z > d + 1), (Z, z == d + 1)):
+            @pl.when((z < Z - 1) & near)
+            def _():
+                zd_copy(d, d, c, below).wait_recv()
+                add_arrived(d, c)
+                zd_copy(d, slot, c, below).start()
+
     for t in range(Z - 1):
-        for c in range(2):
-            up, down = Z - 1 - t, t
-
-            @pl.when((z > 0) & (z < up))
-            def _():
-                zd_copy(up, up, c, lax.rem(z + 1, Z)).wait_recv()
-                add_arrived(up, c)
-                zd_copy(up, up, c, lax.rem(z + 1, Z)).start()
-
-            @pl.when((z < Z - 1) & (z > down + 1))
-            def _():
-                zd_copy(down, down, c, lax.rem(z + Z - 1, Z)).wait_recv()
-                add_arrived(down, c)
-                zd_copy(down, down, c, lax.rem(z + Z - 1, Z)).start()
-
-            @pl.when((z < Z - 1) & (z == down + 1))
-            def _():
-                zd_copy(down, down, c, lax.rem(z + Z - 1, Z)).wait_recv()
-                add_arrived(down, c)
-                zd_copy(down, Z, c, lax.rem(z + Z - 1, Z)).start()
-
-    for q in range(1, E):
-        ret_copy(q).wait_recv()
+        @pl.when(upper == 0)
+        def _():
+            for c in range(2):
+                pass_up(Z - 1 - t, c)
+            for c in range(2):
+                pass_down(t, c)
+
+        @pl.when(upper == 1)
+        def _():
+            for c in range(2):
+                pass_down(t, c)
+            for c in range(2):
+                pass_up(Z - 1 - t, c)
+
+        if t == 0:
+            combine_experts()
 
     @pl.when(z == 0)
     def _():
@@ -350,17 +376,10 @@
         def _():
             zd_copy(z, Z, c, lax.rem(z + 1, Z)).wait_recv()
 
-    trow = min(128, T)
-    residual = pl.ds(pl.multiple_of(z * share, share), share)
     for i in range(T // trow):
         rows = slice(i * trow, (i + 1) * trow)
-        res = jnp.zeros((trow, share), f32)
-        for q in range(E):
-            wanted = slot_col[rows, :] - (expert_at(q // 2, q % 2) * cap).astype(f32)
-            pick = (lax.broadcasted_iota(jnp.int32, (trow, cap), 1).astype(f32) == wanted).astype(f32).astype(bf16)
-            res = res + jnp.dot(pick, rret[q * cap:(q + 1) * cap, :], preferred_element_type=f32)
         dense = pd[z, rows, :].astype(f32) + rpd[z, rows, :].astype(f32) + rpd[Z, rows, :].astype(f32)
-        out[rows, :] = (tok[rows, residual].astype(f32) + dense + gate[rows, :] * res).astype(bf16)
+        out[rows, :] = (base[rows, :] + dense).astype(bf16)
 
     for copy in own_copies:
         copy.wait_send()
@@ -409,6 +428,7 @@
             pltpu.VMEM((Z, E * cap, share), bf16), pltpu.VMEM((Z, E * cap, share), bf16),
             pltpu.VMEM((Z, T, share), bf16), pltpu.VMEM((Z + 1, T, share), bf16),
             pltpu.VMEM((E * cap, share), bf16), pltpu.VMEM((E * cap, share), bf16),
+            pltpu.VMEM((T, share), jnp.float32),
             dma((5,)), dma((2,)), dma((2,)), dma((E,)), dma((E,)),
             dma((2, C, max(SUBS))), dma((2, C, max(SUBS))),
             dma((2, C, max(SUBS), G)), dma((2, C, max(SUBS), G)), dma((2, C, max(SUBS), G)), dma((2, C, max(SUBS), G)),

time: 156 us -> 144 us (0.923)
  the two profiles are of different devices: /device:TPU:20 before, /device:TPU:0 now
where the time goes in v3:
time: 144 us; the launch traced here: 143 us
  Pallas kernels  138 us (96%)
  local copies, waits for them, and re-layouts  4.94 us (3%)
    pallas_call x1, Pallas kernels, local(): pl.pallas_call(functools.partial(kernel, G, E, Z, cap), out_shape=jax.Sha...  138 us
    unnamed x2, local copies, waits for them, and re-layouts  3.4 us

profile of v3, /device:TPU:0, one launch (start us, length us, event | category | flops | bytes accessed | tf_op | source)
XLA Modules:
  0.0 143.3 jit_solution(14794617653891997243)
XLA Ops:
  0.0 1.5 %copy.10.route = s32[512,1]{1,0:T(8,128)} copy(s32[512,1]{0,1:T(1,128)} %param.9) | data formatting | bytes 4096 | tf_op args[1]
  1.5 1.5 %copy.11.gate = f32[512,1]{1,0:T(8,128)} copy(f32[512,1]{0,1:T(1,128)} %bitcast.3) | data formatting | bytes 4096 | tf_op jit(solution)/shard_map/broadcast_in_dim | solution.py:440
  3.1 138.4 %shard_map.82 = bf16[512,512]{1,0:T(8,128)(2,1)} custom-call(bf16[512,2048]{1,0:T(8,128)(2,1)} %tokens.1, s32[512,1]{1,0:T(8,128)} %copy.10.route, f32[512,1]{1,0:T(8,128)} %copy.11.gate, f32[1,2048]{1,0:T(1,128)} %bitcast.2, bf16[512,2048]{1,0:T(8,128)(2,1)} %din.1, bf16[2048,512]{1,0:T(8,128)(2,1)} %dout.1, bf16[1,2048,2048]{2,1,0:T(8,128)(2,1)} %ein_h.1, ...), custom_call_target="tpu_custom_call" | custom-call | tf_op jit(solution)/shard_map/pallas_call | solution.py:417
  141.5 1.9 %copy.13 = bf16[512,512]{1,0:T(8,128)(2,1)} copy(bf16[512,512]{1,0:T(8,128)(2,1)} %shard_map.82) | data formatting | bytes 1048576
